TPU v7x, 32 devices: a whole 2x2x4 slice. The times are simulated.
32 devices in a mesh: row: 4 (over y, core), col: 8 (over z, x).
Axes of the slice: x: 2, y: 2, z: 4, core: 2. Of those that a mesh axis runs over, the one named last changes fastest.
Arguments:
- right_side: float32 [5, 2, 64, 2048], P(None, None, None, 'row'), may hold values from -6 to 6
- panels: float32 [10, 2, 2048, 2048], P(None, None, 'row', 'col'), may hold values from -0.0625 to 0.0625
- diag_inverse: float32 [5, 2, 2048, 2048], P(None, None, 'row', 'col'), may hold values from -0.026516504 to 1.4
- parents: int32 [4, 2], replicated, may hold values from 0 to 1
- live_width: int32 [5, 2], replicated, may hold values from 1024 to 2048
- tile_pattern: int32 [10, 2, 16], replicated, may hold values 0 or 1
Outputs:
- interim: float32 [5, 2, 64, 2048], P(None, None, None, 'row')
- solution: float32 [5, 2, 64, 2048], P(None, None, None, 'row')
Inputs may be any that keep to these rules, and one draw needn't show every extreme that they name: parents[h, k] is the position on level h + 1 of the parent of supernode (h, k). The columns of supernode (h, k) from live_width[h, k] up to 2048 are padding. `tile_pattern`: 1 where the tile of 128 rows is present in the block.
All inputs are finite; a program needn't handle non-finite values.
Results may differ from a plain program's by a relative error of at most 0.0001.
Values sent between devices are 32-bit elements; how exact they have to be, the bound alone decides.
No kernel may reach another device: no remote copies, remote signals or barrier semaphores. Data moves between devices by JAX's collectives and lax.ppermute only.
A program may use at most 64 MiB of HBM per device.

v0:
```python
import jax
import jax.numpy as jnp
from jax import lax
from jax.sharding import PartitionSpec as P

TILE = 128
HIGHEST_PRECISION = lax.Precision.HIGHEST


def pair_index(lower, higher, depth_count):
    return lower * depth_count - lower * (lower + 1) // 2 + (higher - lower - 1)


def climb_maps(parents):
    depth_count = parents.shape[0] + 1
    width_count = parents.shape[1]
    positions = jnp.arange(width_count, dtype=jnp.int32)
    hop_maps = [
        (parents[height][:, None] == positions[None, :]).astype(jnp.float32)
        for height in range(depth_count - 1)
    ]
    climbs = {}
    for height in range(depth_count - 1):
        current = hop_maps[height]
        climbs[height, height + 1] = current
        for higher in range(height + 2, depth_count):
            current = jnp.dot(current, hop_maps[higher - 1], precision=HIGHEST_PRECISION)
            climbs[height, higher] = current
    return climbs


def per_device(right_side, panels, diag_inverse, parents, live_width, tile_pattern):
    levels = right_side.shape[0]
    per_level = right_side.shape[1]
    rhs_count = right_side.shape[2]
    row_span = right_side.shape[3]
    col_span = panels.shape[3]
    row_place = lax.axis_index("row")
    col_place = lax.axis_index("col")
    row_cells = row_place * row_span + jnp.arange(row_span, dtype=jnp.int32)
    col_cells = col_place * col_span + jnp.arange(col_span, dtype=jnp.int32)
    row_live = (row_cells[None, None, :] < live_width[:, :, None]).astype(jnp.float32)
    col_live = (col_cells[None, None, :] < live_width[:, :, None]).astype(jnp.float32)
    tile_count = row_span // TILE
    local_tiles = lax.dynamic_slice_in_dim(tile_pattern, row_place * tile_count, tile_count, 2)
    row_keep = jnp.repeat(local_tiles.astype(jnp.float32), TILE, axis=2)
    climbs = climb_maps(parents)

    def forward_turn(values):
        full_vector = lax.all_gather(values, "row", axis=2, tiled=True)
        return lax.dynamic_slice_in_dim(full_vector, col_place * col_span, col_span, 2)

    def backward_turn(values):
        full_vector = lax.all_gather(values, "col", axis=2, tiled=True)
        return lax.dynamic_slice_in_dim(full_vector, row_place * row_span, row_span, 2)

    pending = [jnp.zeros((per_level, rhs_count, row_span), jnp.float32) for height in range(levels)]
    interim = []
    for height in range(levels):
        if height > 0:
            summed = lax.psum(pending[height], "col")
            residual = right_side[height] - summed
        else:
            residual = right_side[height]
        turned = forward_turn(residual) * col_live[height][:, None, :]
        partial_solve = jnp.einsum(
            "kab,kjb->kja", diag_inverse[height], turned, precision=HIGHEST_PRECISION
        )
        solved = lax.psum(partial_solve, "col") * row_live[height][:, None, :]
        interim.append(solved)
        if height + 1 < levels:
            solved_cols = forward_turn(solved)
            for higher in range(height + 1, levels):
                block_slot = pair_index(height, higher, levels)
                update_term = jnp.einsum(
                    "kab,kjb->kja", panels[block_slot], solved_cols, precision=HIGHEST_PRECISION
                )
                update_term = update_term * row_keep[block_slot][:, None, :]
                pending[higher] = pending[higher] + jnp.einsum(
                    "kt,kja->tja", climbs[height, higher], update_term, precision=HIGHEST_PRECISION
                )
    solution = [None] * levels
    for height in reversed(range(levels)):
        if height + 1 < levels:
            carried = jnp.zeros((per_level, rhs_count, col_span), jnp.float32)
            for higher in range(height + 1, levels):
                block_slot = pair_index(height, higher, levels)
                ancestor_part = jnp.einsum(
                    "kt,tja->kja",
                    climbs[height, higher],
                    solution[higher],
                    precision=HIGHEST_PRECISION,
                )
                ancestor_part = ancestor_part * row_keep[block_slot][:, None, :]
                carried = carried + jnp.einsum(
                    "kab,kja->kjb", panels[block_slot], ancestor_part, precision=HIGHEST_PRECISION
                )
            total_carried = lax.psum(carried, "row")
            remaining = interim[height] - backward_turn(total_carried)
        else:
            remaining = interim[height]
        masked = remaining * row_live[height][:, None, :]
        partial_back = jnp.einsum(
            "kab,kja->kjb", diag_inverse[height], masked, precision=HIGHEST_PRECISION
        )
        back_cols = lax.psum(partial_back, "row") * col_live[height][:, None, :]
        solution[height] = backward_turn(back_cols)
    return (jnp.stack(interim), jnp.stack(solution))


def solution(mesh):
    return jax.shard_map(
        per_device,
        mesh=mesh,
        in_specs=(
            P(None, None, None, "row"),
            P(None, None, "row", "col"),
            P(None, None, "row", "col"),
            P(),
            P(),
            P(),
        ),
        out_specs=(P(None, None, None, "row"), P(None, None, None, "row")),
        check_vma=False,
    )
```

profile of v0, /device:TPU:0, one launch (start us, length us, event | category | flops | bytes accessed | tf_op | source)
XLA Modules:
  0.0 1556.6 jit_solution(9475857177889159699)
XLA Ops:
  9.9 19.7 %all-gather.54.cloned.1.call-done = f32[1,2,64,2048]{3,2,1,0:T(8,128)} async-done(((f32[1,2,64,512]{3,2,1,0:T(8,128)}), f32[1,2,64,2048]{3,2,1,0:T(8,128)}) %all-gather.54.cloned.1.call-update) | async-done | bytes 1048592 | tf_op jit(solution)/shard_map/all_gather | solution.py:50
  29.6 3.1 fusion.42
  32.8 71.7 %all-reduce.19.cloned.1.call-done = f32[2,64,512]{2,1,0:T(8,128)} async-done(((f32[2,64,512]{2,1,0:T(8,128)}), f32[2,64,512]{2,1,0:T(8,128)}) %all-reduce.19.cloned.1.call-update) | async-done | bytes 262160 | tf_op jit(solution)/shard_map/psum | solution.py:69
  108.3 14.4 all-gather.20.cloned.1.call-done
  122.6 2.4 convolution_multiply_fusion.9
  126.8 71.1 %all-reduce.21.cloned.1.call-done = f32[2,64,512]{2,1,0:T(8,128)} async-done(((f32[2,64,512]{2,1,0:T(8,128)}), f32[2,64,512]{2,1,0:T(8,128)}) %all-reduce.21.cloned.1.call-update) | async-done | bytes 262160 | tf_op jit(solution)/shard_map/psum | solution.py:61
  199.6 16.2 %all-gather.22.cloned.1.call-done = f32[2,64,2048]{2,1,0:T(8,128)} async-done(((f32[2,64,512]{2,1,0:T(8,128)}), f32[2,64,2048]{2,1,0:T(8,128)}) %all-gather.22.cloned.1.call-update) | async-done | bytes 1048592 | tf_op jit(solution)/shard_map/all_gather | solution.py:50
  215.8 3.1 fusion.35
  219.0 71.7 %all-reduce.23.cloned.1.call-done = f32[2,64,512]{2,1,0:T(8,128)} async-done(((f32[2,64,512]{2,1,0:T(8,128)}), f32[2,64,512]{2,1,0:T(8,128)}) %all-reduce.23.cloned.1.call-update) | async-done | bytes 262160 | tf_op jit(solution)/shard_map/psum | solution.py:69
  292.7 2.4 convolution_multiply_fusion.8
  296.4 12.0 all-gather.24.cloned.1.call-done
  308.5 2.4 convolution_multiply_fusion.7
  312.6 71.1 %all-reduce.25.cloned.1.call-done = f32[2,64,512]{2,1,0:T(8,128)} async-done(((f32[2,64,512]{2,1,0:T(8,128)}), f32[2,64,512]{2,1,0:T(8,128)}) %all-reduce.25.cloned.1.call-update) | async-done | bytes 262160 | tf_op jit(solution)/shard_map/psum | solution.py:61
  385.5 16.3 %all-gather.26.cloned.1.call-done = f32[2,64,2048]{2,1,0:T(8,128)} async-done(((f32[2,64,512]{2,1,0:T(8,128)}), f32[2,64,2048]{2,1,0:T(8,128)}) %all-gather.26.cloned.1.call-update) | async-done | bytes 1048592 | tf_op jit(solution)/shard_map/all_gather | solution.py:50
  401.8 3.1 fusion.26
  405.1 71.5 %all-reduce.27.cloned.1.call-done = f32[2,64,512]{2,1,0:T(8,128)} async-done(((f32[2,64,512]{2,1,0:T(8,128)}), f32[2,64,512]{2,1,0:T(8,128)}) %all-reduce.27.cloned.1.call-update) | async-done | bytes 262160 | tf_op jit(solution)/shard_map/psum | solution.py:69
  479.4 2.4 convolution_multiply_fusion.6
  483.2 2.5 convolution_multiply_fusion.5
  487.0 7.5 all-gather.28.cloned.1.call-done
  494.5 2.4 convolution_multiply_fusion.4
  498.6 71.1 %all-reduce.29.cloned.1.call-done = f32[2,64,512]{2,1,0:T(8,128)} async-done(((f32[2,64,512]{2,1,0:T(8,128)}), f32[2,64,512]{2,1,0:T(8,128)}) %all-reduce.29.cloned.1.call-update) | async-done | bytes 262160 | tf_op jit(solution)/shard_map/psum | solution.py:61
  571.5 16.3 %all-gather.30.cloned.1.call-done = f32[2,64,2048]{2,1,0:T(8,128)} async-done(((f32[2,64,512]{2,1,0:T(8,128)}), f32[2,64,2048]{2,1,0:T(8,128)}) %all-gather.30.cloned.1.call-update) | async-done | bytes 1048592 | tf_op jit(solution)/shard_map/all_gather | solution.py:50
  587.9 3.1 fusion.15
  591.5 71.2 %all-reduce.31.cloned.1.call-done = f32[2,64,512]{2,1,0:T(8,128)} async-done(((f32[2,64,512]{2,1,0:T(8,128)}), f32[2,64,512]{2,1,0:T(8,128)}) %all-reduce.31.cloned.1.call-update) | async-done | bytes 262160 | tf_op jit(solution)/shard_map/psum | solution.py:69
  664.9 2.4 convolution_multiply_fusion.3
  668.6 2.5 convolution_multiply_fusion.2
  672.4 2.4 convolution_multiply_fusion.1
  676.1 4.4 all-gather.32.cloned.1.call-done
  680.5 2.4 convolution_multiply_fusion
  684.8 71.1 %all-reduce.33.cloned.1.call-done = f32[2,64,512]{2,1,0:T(8,128)} async-done(((f32[2,64,512]{2,1,0:T(8,128)}), f32[2,64,512]{2,1,0:T(8,128)}) %all-reduce.33.cloned.1.call-update) | async-done | bytes 262160 | tf_op jit(solution)/shard_map/psum | solution.py:61
  757.7 16.0 %all-gather.34.cloned.1.call-done = f32[2,64,2048]{2,1,0:T(8,128)} async-done(((f32[2,64,512]{2,1,0:T(8,128)}), f32[2,64,2048]{2,1,0:T(8,128)}) %all-gather.34.cloned.1.call-update) | async-done | bytes 1048592 | tf_op jit(solution)/shard_map/all_gather | solution.py:50
  773.7 3.1 fusion.2
  776.9 71.1 %all-reduce.35.cloned.1.call-done = f32[2,64,512]{2,1,0:T(8,128)} async-done(((f32[2,64,512]{2,1,0:T(8,128)}), f32[2,64,512]{2,1,0:T(8,128)}) %all-reduce.35.cloned.1.call-update) | async-done | bytes 262160 | tf_op jit(solution)/shard_map/psum | solution.py:69
  848.0 2.8 fusion
  850.9 31.1 %all-reduce.37.cloned.1.call-done = f32[2,64,256]{2,1,0:T(8,128)} async-done(((f32[2,64,256]{2,1,0:T(8,128)}), f32[2,64,256]{2,1,0:T(8,128)}) %all-reduce.37.cloned.1.call-update) | async-done | bytes 131088 | tf_op jit(solution)/shard_map/psum | solution.py:106
  883.6 39.7 %all-gather.36.cloned.1.call-done = f32[2,64,2048]{2,1,0:T(8,128)} async-done(((f32[2,64,256]{2,1,0:T(8,128)}), f32[2,64,2048]{2,1,0:T(8,128)}) %all-gather.36.cloned.1.call-update) | async-done | bytes 1048592 | tf_op jit(solution)/shard_map/all_gather | solution.py:54
  924.9 2.7 fusion.4
  927.7 30.9 %all-reduce.39.cloned.1.call-done = f32[2,64,256]{2,1,0:T(8,128)} async-done(((f32[2,64,256]{2,1,0:T(8,128)}), f32[2,64,256]{2,1,0:T(8,128)}) %all-reduce.39.cloned.1.call-update) | async-done | bytes 131088 | tf_op jit(solution)/shard_map/psum | solution.py:98
  958.9 41.2 %all-gather.38.cloned.1.call-done = f32[2,64,2048]{2,1,0:T(8,128)} async-done(((f32[2,64,256]{2,1,0:T(8,128)}), f32[2,64,2048]{2,1,0:T(8,128)}) %all-gather.38.cloned.1.call-update) | async-done | bytes 1048592 | tf_op jit(solution)/shard_map/all_gather | solution.py:54
  1000.1 2.8 fusion.13
  1002.9 30.9 %all-reduce.41.cloned.1.call-done = f32[2,64,256]{2,1,0:T(8,128)} async-done(((f32[2,64,256]{2,1,0:T(8,128)}), f32[2,64,256]{2,1,0:T(8,128)}) %all-reduce.41.cloned.1.call-update) | async-done | bytes 131088 | tf_op jit(solution)/shard_map/psum | solution.py:106
  1036.6 38.6 %all-gather.40.cloned.1.call-done = f32[2,64,2048]{2,1,0:T(8,128)} async-done(((f32[2,64,256]{2,1,0:T(8,128)}), f32[2,64,2048]{2,1,0:T(8,128)}) %all-gather.40.cloned.1.call-update) | async-done | bytes 1048592 | tf_op jit(solution)/shard_map/all_gather | solution.py:54
  1076.8 2.0 fusion.17
  1078.9 2.7 convolution_add_fusion.5
  1081.7 30.9 %all-reduce.43.cloned.1.call-done = f32[2,64,256]{2,1,0:T(8,128)} async-done(((f32[2,64,256]{2,1,0:T(8,128)}), f32[2,64,256]{2,1,0:T(8,128)}) %all-reduce.43.cloned.1.call-update) | async-done | bytes 131088 | tf_op jit(solution)/shard_map/psum | solution.py:98
  1112.7 41.2 %all-gather.42.cloned.1.call-done = f32[2,64,2048]{2,1,0:T(8,128)} async-done(((f32[2,64,256]{2,1,0:T(8,128)}), f32[2,64,2048]{2,1,0:T(8,128)}) %all-gather.42.cloned.1.call-update) | async-done | bytes 1048592 | tf_op jit(solution)/shard_map/all_gather | solution.py:54
  1153.9 2.8 fusion.24
  1156.8 30.9 %all-reduce.45.cloned.1.call-done = f32[2,64,256]{2,1,0:T(8,128)} async-done(((f32[2,64,256]{2,1,0:T(8,128)}), f32[2,64,256]{2,1,0:T(8,128)}) %all-reduce.45.cloned.1.call-update) | async-done | bytes 131088 | tf_op jit(solution)/shard_map/psum | solution.py:106
  1191.5 37.6 %all-gather.44.cloned.1.call-done = f32[2,64,2048]{2,1,0:T(8,128)} async-done(((f32[2,64,256]{2,1,0:T(8,128)}), f32[2,64,2048]{2,1,0:T(8,128)}) %all-gather.44.cloned.1.call-update) | async-done | bytes 1048592 | tf_op jit(solution)/shard_map/all_gather | solution.py:54
  1232.9 2.0 convolution_add_fusion.4
  1234.9 2.7 convolution_add_fusion.3
  1237.7 30.9 %all-reduce.47.cloned.1.call-done = f32[2,64,256]{2,1,0:T(8,128)} async-done(((f32[2,64,256]{2,1,0:T(8,128)}), f32[2,64,256]{2,1,0:T(8,128)}) %all-reduce.47.cloned.1.call-update) | async-done | bytes 131088 | tf_op jit(solution)/shard_map/psum | solution.py:98
  1268.7 41.2 %all-gather.46.cloned.1.call-done = f32[2,64,2048]{2,1,0:T(8,128)} async-done(((f32[2,64,256]{2,1,0:T(8,128)}), f32[2,64,2048]{2,1,0:T(8,128)}) %all-gather.46.cloned.1.call-update) | async-done | bytes 1048592 | tf_op jit(solution)/shard_map/all_gather | solution.py:54
  1309.9 2.8 fusion.33
  1312.7 30.9 %all-reduce.49.cloned.1.call-done = f32[2,64,256]{2,1,0:T(8,128)} async-done(((f32[2,64,256]{2,1,0:T(8,128)}), f32[2,64,256]{2,1,0:T(8,128)}) %all-reduce.49.cloned.1.call-update) | async-done | bytes 131088 | tf_op jit(solution)/shard_map/psum | solution.py:106
  1348.8 36.3 %all-gather.48.cloned.1.call-done = f32[2,64,2048]{2,1,0:T(8,128)} async-done(((f32[2,64,256]{2,1,0:T(8,128)}), f32[2,64,2048]{2,1,0:T(8,128)}) %all-gather.48.cloned.1.call-update) | async-done | bytes 1048592 | tf_op jit(solution)/shard_map/all_gather | solution.py:54
  1388.8 2.0 convolution_add_fusion.2
  1390.8 2.0 convolution_add_fusion.1
  1392.9 2.7 convolution_add_fusion
  1395.6 30.9 %all-reduce.51.cloned.1.call-done = f32[2,64,256]{2,1,0:T(8,128)} async-done(((f32[2,64,256]{2,1,0:T(8,128)}), f32[2,64,256]{2,1,0:T(8,128)}) %all-reduce.51.cloned.1.call-update) | async-done | bytes 131088 | tf_op jit(solution)/shard_map/psum | solution.py:98
  1426.6 41.4 %all-gather.50.cloned.1.call-done = f32[2,64,2048]{2,1,0:T(8,128)} async-done(((f32[2,64,256]{2,1,0:T(8,128)}), f32[2,64,2048]{2,1,0:T(8,128)}) %all-gather.50.cloned.1.call-update) | async-done | bytes 1048592 | tf_op jit(solution)/shard_map/all_gather | solution.py:54
  1468.0 2.8 fusion.40
  1470.9 30.9 %all-reduce.53.cloned.1.call-done = f32[2,64,256]{2,1,0:T(8,128)} async-done(((f32[2,64,256]{2,1,0:T(8,128)}), f32[2,64,256]{2,1,0:T(8,128)}) %all-reduce.53.cloned.1.call-update) | async-done | bytes 131088 | tf_op jit(solution)/shard_map/psum | solution.py:106
  1504.1 39.5 %all-gather.52.cloned.1.call-done = f32[2,64,2048]{2,1,0:T(8,128)} async-done(((f32[2,64,256]{2,1,0:T(8,128)}), f32[2,64,2048]{2,1,0:T(8,128)}) %all-gather.52.cloned.1.call-update) | async-done | bytes 1048592 | tf_op jit(solution)/shard_map/all_gather | solution.py:54
  (170 shorter events, 69.3 us)
Async XLA Ops:
  7.2 190.7 %copy-start.4 = (f32[5,2,64,512]{3,2,1,0:T(8,128)S(1)}, f32[5,2,64,512]{3,2,1,0:T(8,128)}, u32[]{:S(2)}) copy-start(f32[5,2,64,512]{3,2,1,0:T(8,128)} %param.6) | copy-start | bytes 3932164
  7.2 22.4 %all-gather.54.cloned.1.call-start = ((), (), s32[]{:S(2)}) async-start(), calls=%async_computation.35 | async-start | bytes 1310720 | tf_op jit(solution)/shard_map/all_gather | solution.py:50
  9.0 95.6 %all-reduce.19.cloned.1.call-start = ((), (), s32[]{:S(2)}) async-start(), calls=%async_computation | async-start | bytes 524288 | tf_op jit(solution)/shard_map/psum | solution.py:69
  32.7 89.9 %all-gather.20.cloned.1.call-start = ((), (), s32[]{:S(2)}) async-start(), calls=%async_computation.1 | async-start | bytes 1310720 | tf_op jit(solution)/shard_map/all_gather | solution.py:50
  106.3 91.6 %all-reduce.21.cloned.1.call-start = ((), (), s32[]{:S(2)}) async-start(), calls=%async_computation.2 | async-start | bytes 524288 | tf_op jit(solution)/shard_map/psum | solution.py:61
  126.7 89.1 %all-gather.22.cloned.1.call-start = ((), (), s32[]{:S(2)}) async-start(), calls=%async_computation.3 | async-start | bytes 1310720 | tf_op jit(solution)/shard_map/all_gather | solution.py:50
  199.6 91.0 %all-reduce.23.cloned.1.call-start = ((), (), s32[]{:S(2)}) async-start(), calls=%async_computation.4 | async-start | bytes 524288 | tf_op jit(solution)/shard_map/psum | solution.py:69
  218.9 89.5 %all-gather.24.cloned.1.call-start = ((), (), s32[]{:S(2)}) async-start(), calls=%async_computation.5 | async-start | bytes 1310720 | tf_op jit(solution)/shard_map/all_gather | solution.py:50
  292.4 91.3 %all-reduce.25.cloned.1.call-start = ((), (), s32[]{:S(2)}) async-start(), calls=%async_computation.6 | async-start | bytes 524288 | tf_op jit(solution)/shard_map/psum | solution.py:61
  312.6 89.3 %all-gather.26.cloned.1.call-start = ((), (), s32[]{:S(2)}) async-start(), calls=%async_computation.7 | async-start | bytes 1310720 | tf_op jit(solution)/shard_map/all_gather | solution.py:50
  385.4 91.2 %all-reduce.27.cloned.1.call-start = ((), (), s32[]{:S(2)}) async-start(), calls=%async_computation.8 | async-start | bytes 524288 | tf_op jit(solution)/shard_map/psum | solution.py:69
  404.9 89.5 %all-gather.28.cloned.1.call-start = ((), (), s32[]{:S(2)}) async-start(), calls=%async_computation.9 | async-start | bytes 1310720 | tf_op jit(solution)/shard_map/all_gather | solution.py:50
  478.4 91.4 %all-reduce.29.cloned.1.call-start = ((), (), s32[]{:S(2)}) async-start(), calls=%async_computation.10 | async-start | bytes 524288 | tf_op jit(solution)/shard_map/psum | solution.py:61
  498.6 89.3 %all-gather.30.cloned.1.call-start = ((), (), s32[]{:S(2)}) async-start(), calls=%async_computation.11 | async-start | bytes 1310720 | tf_op jit(solution)/shard_map/all_gather | solution.py:50
  571.5 91.2 %all-reduce.31.cloned.1.call-start = ((), (), s32[]{:S(2)}) async-start(), calls=%async_computation.12 | async-start | bytes 524288 | tf_op jit(solution)/shard_map/psum | solution.py:69
  591.0 89.5 %all-gather.32.cloned.1.call-start = ((), (), s32[]{:S(2)}) async-start(), calls=%async_computation.13 | async-start | bytes 1310720 | tf_op jit(solution)/shard_map/all_gather | solution.py:50
  664.4 4.2 copy-start.6
  664.4 91.5 %all-reduce.33.cloned.1.call-start = ((), (), s32[]{:S(2)}) async-start(), calls=%async_computation.14 | async-start | bytes 524288 | tf_op jit(solution)/shard_map/psum | solution.py:61
  680.5 319.6 %copy-start.3 = (f32[2,64,512]{2,1,0:T(8,128)S(1)}, f32[2,64,512]{2,1,0:T(8,128)}, u32[]{:S(2)}) copy-start(f32[2,64,512]{2,1,0:T(8,128)} %get-tuple-element.7) | copy-start | bytes 786436
  684.7 89.0 %all-gather.34.cloned.1.call-start = ((), (), s32[]{:S(2)}) async-start(), calls=%async_computation.15 | async-start | bytes 1310720 | tf_op jit(solution)/shard_map/all_gather | solution.py:50
  757.6 90.4 %all-reduce.35.cloned.1.call-start = ((), (), s32[]{:S(2)}) async-start(), calls=%async_computation.16 | async-start | bytes 524288 | tf_op jit(solution)/shard_map/psum | solution.py:69
  776.8 105.1 %all-reduce.37.cloned.1.call-start = ((), (), s32[]{:S(2)}) async-start(), calls=%async_computation.17 | async-start | bytes 262144 | tf_op jit(solution)/shard_map/psum | solution.py:106
  850.8 303.1 %copy-start.2 = (f32[2,64,512]{2,1,0:T(8,128)S(1)}, f32[2,64,512]{2,1,0:T(8,128)}, u32[]{:S(2)}) copy-start(f32[2,64,512]{2,1,0:T(8,128)} %get-tuple-element.9) | copy-start | bytes 786436
  850.8 72.4 %all-gather.36.cloned.1.call-start = ((), (), s32[]{:S(2)}) async-start(), calls=%async_computation.18 | async-start | bytes 1179648 | tf_op jit(solution)/shard_map/all_gather | solution.py:54
  883.5 75.1 %all-reduce.39.cloned.1.call-start = ((), (), s32[]{:S(2)}) async-start(), calls=%async_computation.19 | async-start | bytes 262144 | tf_op jit(solution)/shard_map/psum | solution.py:98
  927.6 72.4 %all-gather.38.cloned.1.call-start = ((), (), s32[]{:S(2)}) async-start(), calls=%async_computation.20 | async-start | bytes 1179648 | tf_op jit(solution)/shard_map/all_gather | solution.py:54
  958.6 75.2 %all-reduce.41.cloned.1.call-start = ((), (), s32[]{:S(2)}) async-start(), calls=%async_computation.21 | async-start | bytes 262144 | tf_op jit(solution)/shard_map/psum | solution.py:106
  1002.9 72.3 %all-gather.40.cloned.1.call-start = ((), (), s32[]{:S(2)}) async-start(), calls=%async_computation.22 | async-start | bytes 1179648 | tf_op jit(solution)/shard_map/all_gather | solution.py:54
  1035.4 77.2 %all-reduce.43.cloned.1.call-start = ((), (), s32[]{:S(2)}) async-start(), calls=%async_computation.23 | async-start | bytes 262144 | tf_op jit(solution)/shard_map/psum | solution.py:98
  1078.9 231.0 %copy-start.1 = (f32[2,64,512]{2,1,0:T(8,128)S(1)}, f32[2,64,512]{2,1,0:T(8,128)}, u32[]{:S(2)}) copy-start(f32[2,64,512]{2,1,0:T(8,128)} %get-tuple-element.11) | copy-start | bytes 786436
  1081.6 72.3 %all-gather.42.cloned.1.call-start = ((), (), s32[]{:S(2)}) async-start(), calls=%async_computation.24 | async-start | bytes 1179648 | tf_op jit(solution)/shard_map/all_gather | solution.py:54
  1112.6 75.1 %all-reduce.45.cloned.1.call-start = ((), (), s32[]{:S(2)}) async-start(), calls=%async_computation.25 | async-start | bytes 262144 | tf_op jit(solution)/shard_map/psum | solution.py:106
  1156.7 72.4 %all-gather.44.cloned.1.call-start = ((), (), s32[]{:S(2)}) async-start(), calls=%async_computation.26 | async-start | bytes 1179648 | tf_op jit(solution)/shard_map/all_gather | solution.py:54
  1189.3 79.3 %all-reduce.47.cloned.1.call-start = ((), (), s32[]{:S(2)}) async-start(), calls=%async_computation.27 | async-start | bytes 262144 | tf_op jit(solution)/shard_map/psum | solution.py:98
  1237.6 72.3 %all-gather.46.cloned.1.call-start = ((), (), s32[]{:S(2)}) async-start(), calls=%async_computation.28 | async-start | bytes 1179648 | tf_op jit(solution)/shard_map/all_gather | solution.py:54
  1268.6 199.4 %copy-start = (f32[2,64,512]{2,1,0:T(8,128)S(1)}, f32[2,64,512]{2,1,0:T(8,128)}, u32[]{:S(2)}) copy-start(f32[2,64,512]{2,1,0:T(8,128)} %get-tuple-element.13) | copy-start | bytes 786436
  1268.6 75.0 %all-reduce.49.cloned.1.call-start = ((), (), s32[]{:S(2)}) async-start(), calls=%async_computation.29 | async-start | bytes 262144 | tf_op jit(solution)/shard_map/psum | solution.py:106
  1312.7 72.4 %all-gather.48.cloned.1.call-start = ((), (), s32[]{:S(2)}) async-start(), calls=%async_computation.30 | async-start | bytes 1179648 | tf_op jit(solution)/shard_map/all_gather | solution.py:54
  1345.2 81.3 %all-reduce.51.cloned.1.call-start = ((), (), s32[]{:S(2)}) async-start(), calls=%async_computation.31 | async-start | bytes 262144 | tf_op jit(solution)/shard_map/psum | solution.py:98
  1347.7 155.7 %copy-start.5 = (f32[2,64,512]{2,1,0:T(8,128)S(1)}, f32[2,64,512]{2,1,0:T(8,128)}, u32[]{:S(2)}) copy-start(f32[2,64,512]{2,1,0:T(8,128)} %all-reduce.35.cloned.1.call-done) | copy-start | bytes 786436
  1395.6 72.4 %all-gather.50.cloned.1.call-start = ((), (), s32[]{:S(2)}) async-start(), calls=%async_computation.32 | async-start | bytes 1179648 | tf_op jit(solution)/shard_map/all_gather | solution.py:54
  1426.6 75.2 %all-reduce.53.cloned.1.call-start = ((), (), s32[]{:S(2)}) async-start(), calls=%async_computation.33 | async-start | bytes 262144 | tf_op jit(solution)/shard_map/psum | solution.py:106
  1470.8 72.8 %all-gather.52.cloned.1.call-start = ((), (), s32[]{:S(2)}) async-start(), calls=%async_computation.34 | async-start | bytes 1179648 | tf_op jit(solution)/shard_map/all_gather | solution.py:54
  1548.5 1.1 copy-start.7
Sparse Core Ops, SparseCore 0:
  10.1 19.4 all-gather.53
  33.5 71.0 all-reduce.18
  106.7 15.8 all-gather.19
  126.8 71.0 all-reduce.20
  199.9 15.8 all-gather.21
  219.6 71.0 all-reduce.22
  292.5 15.8 all-gather.23
  312.7 71.0 all-reduce.24
  385.9 15.8 all-gather.25
  405.6 71.0 all-reduce.26
  478.5 15.8 all-gather.27
  498.7 71.0 all-reduce.28
  571.9 15.8 all-gather.29
  591.6 71.0 all-reduce.30
  664.6 15.8 all-gather.31
  684.8 71.0 all-reduce.32
  757.8 15.8 all-gather.33
  777.0 71.0 all-reduce.34
  850.9 30.9 all-reduce.36
  883.8 39.3 all-gather.35
  927.8 30.7 all-reduce.38
  960.7 39.3 all-gather.37
  1003.0 30.7 all-reduce.40
  1035.7 39.3 all-gather.39
  1081.7 30.7 all-reduce.42
  1114.5 39.3 all-gather.41
  1156.8 30.7 all-reduce.44
  1189.7 39.3 all-gather.43
  1237.7 30.7 all-reduce.46
  1270.5 39.3 all-gather.45
  1312.8 30.7 all-reduce.48
  1345.7 39.3 all-gather.47
  1395.7 30.7 all-reduce.50
  1428.6 39.3 all-gather.49
  1470.9 30.7 all-reduce.52
  1504.2 39.3 all-gather.51
where the time goes:
time: 1570 us; the launch traced here: 1560 us
  waiting for transfers between devices  1400 us (89%)
  matrix products  98.3 us (6%)
  other arithmetic  25.7 us (2%)
    psum x5, waiting for transfers between devices, per_device(): solved = lax.psum(partial_solve, 'col') * row_live[height][:, None, :]  357 us
    all_gather x9, waiting for transfers between devices, backward_turn(): full_vector = lax.all_gather(values, 'col', axis=2, tiled=True)  357 us
    psum x4, waiting for transfers between devices, per_device(): summed = lax.psum(pending[height], 'col')  285 us
    psum x5, waiting for transfers between devices, per_device(): back_cols = lax.psum(partial_back, 'row') * col_live[height][:, None, :]  155 us
    psum x4, waiting for transfers between devices, per_device(): total_carried = lax.psum(carried, 'row')  124 us
    all_gather x9, waiting for transfers between devices, forward_turn(): full_vector = lax.all_gather(values, 'row', axis=2, tiled=True)  123 us
  transfers between devices with their start and end apart: 36, of which 36 were waited for; matrix products, arithmetic and copies ran while one was open for 2% of the time, Pallas kernels for 0%

commit v1 on v0

--- a/solution.py
+++ b/solution.py
@@ -58,7 +58,7 @@
     interim = []
     for height in range(levels):
         if height > 0:
-            summed = lax.psum(pending[height], "col")
+            summed = jnp.sum(lax.all_gather(pending[height], "col"), axis=0)
             residual = right_side[height] - summed
         else:
             residual = right_side[height]

time: 1570 us -> 1480 us (0.943)
  waiting for transfers between devices: 1400 us -> 1310 us
    psum x4 -> x0, waiting for transfers between devices: 285 us -> none  [per_device(): summed = lax.psum(pending[height], 'col')]
    all_gather x0 -> x4, waiting for transfers between devices: none -> 197 us  [per_device(): summed = jnp.sum(lax.all_gather(pending[height], 'col'), axis=0)]
where the time goes in v1:
time: 1480 us; the launch traced here: 1470 us
  waiting for transfers between devices  1310 us (89%)
  matrix products  98 us (7%)
  other arithmetic  25.9 us (2%)
  local copies, waits for them, and re-layouts  17.1 us (1%)
  between operations  14.8 us (1%)
    all_gather x9, waiting for transfers between devices, backward_turn(): full_vector = lax.all_gather(values, 'col', axis=2, tiled=True)  358 us
    psum x5, waiting for transfers between devices, per_device(): solved = lax.psum(partial_solve, 'col') * row_live[height][:, None, :]  356 us
    all_gather x4, waiting for transfers between devices, per_device(): summed = jnp.sum(lax.all_gather(pending[height], 'col'), axis=0)  197 us
    psum x5, waiting for transfers between devices, per_device(): back_cols = lax.psum(partial_back, 'row') * col_live[height][:, None, :]  155 us
    psum x4, waiting for transfers between devices, per_device(): total_carried = lax.psum(carried, 'row')  124 us
    all_gather x9, waiting for transfers between devices, forward_turn(): full_vector = lax.all_gather(values, 'row', axis=2, tiled=True)  123 us
  transfers between devices with their start and end apart: 36, of which 36 were waited for; matrix products, arithmetic and copies ran while one was open for 2% of the time, Pallas kernels for 0%

profile of v1, /device:TPU:0, one launch (start us, length us, event | category | flops | bytes accessed | tf_op | source)
XLA Modules:
  0.0 1471.8 jit_solution(5883004477351945266)
XLA Ops:
  9.9 19.7 %all-gather.62.cloned.1.call-done = f32[1,2,64,2048]{3,2,1,0:T(8,128)} async-done(((f32[1,2,64,512]{3,2,1,0:T(8,128)}), f32[1,2,64,2048]{3,2,1,0:T(8,128)}) %all-gather.62.cloned.1.call-update) | async-done | bytes 1048592 | tf_op jit(solution)/shard_map/all_gather | solution.py:50
  29.6 3.1 fusion.54
  32.8 71.7 %all-reduce.15.cloned.1.call-done = f32[2,64,512]{2,1,0:T(8,128)} async-done(((f32[2,64,512]{2,1,0:T(8,128)}), f32[2,64,512]{2,1,0:T(8,128)}) %all-reduce.15.cloned.1.call-update) | async-done | bytes 262160 | tf_op jit(solution)/shard_map/psum | solution.py:69
  108.3 14.4 all-gather.28.cloned.1.call-done
  122.6 2.4 fusion.50
  126.6 49.2 %all-gather.64.cloned.1.call-done = f32[16,64,512]{2,1,0:T(8,128)} async-done(((f32[2,64,512]{2,1,0:T(8,128)}), f32[16,64,512]{2,1,0:T(8,128)}) %all-gather.64.cloned.1.call-update) | async-done | bytes 2097168 | tf_op jit(solution)/shard_map/all_gather | solution.py:61
  178.4 15.3 %all-gather.30.cloned.1.call-done = f32[2,64,2048]{2,1,0:T(8,128)} async-done(((f32[2,64,512]{2,1,0:T(8,128)}), f32[2,64,2048]{2,1,0:T(8,128)}) %all-gather.30.cloned.1.call-update) | async-done | bytes 1048592 | tf_op jit(solution)/shard_map/all_gather | solution.py:50
  193.8 3.1 fusion.46
  197.0 71.6 %all-reduce.17.cloned.1.call-done = f32[2,64,512]{2,1,0:T(8,128)} async-done(((f32[2,64,512]{2,1,0:T(8,128)}), f32[2,64,512]{2,1,0:T(8,128)}) %all-reduce.17.cloned.1.call-update) | async-done | bytes 262160 | tf_op jit(solution)/shard_map/psum | solution.py:69
  270.7 2.4 fusion.42
  273.2 13.5 all-gather.32.cloned.1.call-done
  286.7 2.4 fusion.39
  292.0 49.2 %all-gather.66.cloned.1.call-done = f32[16,64,512]{2,1,0:T(8,128)} async-done(((f32[2,64,512]{2,1,0:T(8,128)}), f32[16,64,512]{2,1,0:T(8,128)}) %all-gather.66.cloned.1.call-update) | async-done | bytes 2097168 | tf_op jit(solution)/shard_map/all_gather | solution.py:61
  343.8 15.3 %all-gather.34.cloned.1.call-done = f32[2,64,2048]{2,1,0:T(8,128)} async-done(((f32[2,64,512]{2,1,0:T(8,128)}), f32[2,64,2048]{2,1,0:T(8,128)}) %all-gather.34.cloned.1.call-update) | async-done | bytes 1048592 | tf_op jit(solution)/shard_map/all_gather | solution.py:50
  359.2 3.1 fusion.35
  362.4 71.0 %all-reduce.19.cloned.1.call-done = f32[2,64,512]{2,1,0:T(8,128)} async-done(((f32[2,64,512]{2,1,0:T(8,128)}), f32[2,64,512]{2,1,0:T(8,128)}) %all-reduce.19.cloned.1.call-update) | async-done | bytes 262160 | tf_op jit(solution)/shard_map/psum | solution.py:69
  435.9 2.4 fusion.31
  439.7 2.5 fusion.28
  442.1 9.2 all-gather.36.cloned.1.call-done
  451.3 2.4 fusion.25
  456.6 49.2 %all-gather.68.cloned.1.call-done = f32[16,64,512]{2,1,0:T(8,128)} async-done(((f32[2,64,512]{2,1,0:T(8,128)}), f32[16,64,512]{2,1,0:T(8,128)}) %all-gather.68.cloned.1.call-update) | async-done | bytes 2097168 | tf_op jit(solution)/shard_map/all_gather | solution.py:61
  508.5 15.3 %all-gather.38.cloned.1.call-done = f32[2,64,2048]{2,1,0:T(8,128)} async-done(((f32[2,64,512]{2,1,0:T(8,128)}), f32[2,64,2048]{2,1,0:T(8,128)}) %all-gather.38.cloned.1.call-update) | async-done | bytes 1048592 | tf_op jit(solution)/shard_map/all_gather | solution.py:50
  523.8 3.1 fusion.21
  527.2 70.9 %all-reduce.21.cloned.1.call-done = f32[2,64,512]{2,1,0:T(8,128)} async-done(((f32[2,64,512]{2,1,0:T(8,128)}), f32[2,64,512]{2,1,0:T(8,128)}) %all-reduce.21.cloned.1.call-update) | async-done | bytes 262160 | tf_op jit(solution)/shard_map/psum | solution.py:69
  600.5 2.4 fusion.17
  604.3 2.5 fusion.14
  608.1 2.4 fusion.11
  610.5 5.4 all-gather.40.cloned.1.call-done
  615.9 2.4 fusion.8
  621.3 49.2 %all-gather.70.cloned.1.call-done = f32[16,64,512]{2,1,0:T(8,128)} async-done(((f32[2,64,512]{2,1,0:T(8,128)}), f32[16,64,512]{2,1,0:T(8,128)}) %all-gather.70.cloned.1.call-update) | async-done | bytes 2097168 | tf_op jit(solution)/shard_map/all_gather | solution.py:61
  673.1 15.3 %all-gather.42.cloned.1.call-done = f32[2,64,2048]{2,1,0:T(8,128)} async-done(((f32[2,64,512]{2,1,0:T(8,128)}), f32[2,64,2048]{2,1,0:T(8,128)}) %all-gather.42.cloned.1.call-update) | async-done | bytes 1048592 | tf_op jit(solution)/shard_map/all_gather | solution.py:50
  688.4 3.1 fusion.4
  691.6 71.1 %all-reduce.23.cloned.1.call-done = f32[2,64,512]{2,1,0:T(8,128)} async-done(((f32[2,64,512]{2,1,0:T(8,128)}), f32[2,64,512]{2,1,0:T(8,128)}) %all-reduce.23.cloned.1.call-update) | async-done | bytes 262160 | tf_op jit(solution)/shard_map/psum | solution.py:69
  762.7 2.8 fusion.2
  765.5 31.1 %all-reduce.25.cloned.1.call-done = f32[2,64,256]{2,1,0:T(8,128)} async-done(((f32[2,64,256]{2,1,0:T(8,128)}), f32[2,64,256]{2,1,0:T(8,128)}) %all-reduce.25.cloned.1.call-update) | async-done | bytes 131088 | tf_op jit(solution)/shard_map/psum | solution.py:106
  798.2 39.7 %all-gather.44.cloned.1.call-done = f32[2,64,2048]{2,1,0:T(8,128)} async-done(((f32[2,64,256]{2,1,0:T(8,128)}), f32[2,64,2048]{2,1,0:T(8,128)}) %all-gather.44.cloned.1.call-update) | async-done | bytes 1048592 | tf_op jit(solution)/shard_map/all_gather | solution.py:54
  839.7 2.7 fusion.6
  842.4 30.9 %all-reduce.27.cloned.1.call-done = f32[2,64,256]{2,1,0:T(8,128)} async-done(((f32[2,64,256]{2,1,0:T(8,128)}), f32[2,64,256]{2,1,0:T(8,128)}) %all-reduce.27.cloned.1.call-update) | async-done | bytes 131088 | tf_op jit(solution)/shard_map/psum | solution.py:98
  873.8 41.0 %all-gather.46.cloned.1.call-done = f32[2,64,2048]{2,1,0:T(8,128)} async-done(((f32[2,64,256]{2,1,0:T(8,128)}), f32[2,64,2048]{2,1,0:T(8,128)}) %all-gather.46.cloned.1.call-update) | async-done | bytes 1048592 | tf_op jit(solution)/shard_map/all_gather | solution.py:54
  914.8 2.8 fusion.19
  917.6 30.9 %all-reduce.29.cloned.1.call-done = f32[2,64,256]{2,1,0:T(8,128)} async-done(((f32[2,64,256]{2,1,0:T(8,128)}), f32[2,64,256]{2,1,0:T(8,128)}) %all-reduce.29.cloned.1.call-update) | async-done | bytes 131088 | tf_op jit(solution)/shard_map/psum | solution.py:106
  951.3 38.6 %all-gather.48.cloned.1.call-done = f32[2,64,2048]{2,1,0:T(8,128)} async-done(((f32[2,64,256]{2,1,0:T(8,128)}), f32[2,64,2048]{2,1,0:T(8,128)}) %all-gather.48.cloned.1.call-update) | async-done | bytes 1048592 | tf_op jit(solution)/shard_map/all_gather | solution.py:54
  991.7 2.0 fusion.23
  993.7 2.7 convolution_add_fusion.9
  996.5 30.9 %all-reduce.31.cloned.1.call-done = f32[2,64,256]{2,1,0:T(8,128)} async-done(((f32[2,64,256]{2,1,0:T(8,128)}), f32[2,64,256]{2,1,0:T(8,128)}) %all-reduce.31.cloned.1.call-update) | async-done | bytes 131088 | tf_op jit(solution)/shard_map/psum | solution.py:98
  1027.5 41.2 %all-gather.50.cloned.1.call-done = f32[2,64,2048]{2,1,0:T(8,128)} async-done(((f32[2,64,256]{2,1,0:T(8,128)}), f32[2,64,2048]{2,1,0:T(8,128)}) %all-gather.50.cloned.1.call-update) | async-done | bytes 1048592 | tf_op jit(solution)/shard_map/all_gather | solution.py:54
  1068.7 2.8 fusion.33
  1071.5 30.9 %all-reduce.33.cloned.1.call-done = f32[2,64,256]{2,1,0:T(8,128)} async-done(((f32[2,64,256]{2,1,0:T(8,128)}), f32[2,64,256]{2,1,0:T(8,128)}) %all-reduce.33.cloned.1.call-update) | async-done | bytes 131088 | tf_op jit(solution)/shard_map/psum | solution.py:106
  1106.3 37.7 %all-gather.52.cloned.1.call-done = f32[2,64,2048]{2,1,0:T(8,128)} async-done(((f32[2,64,256]{2,1,0:T(8,128)}), f32[2,64,2048]{2,1,0:T(8,128)}) %all-gather.52.cloned.1.call-update) | async-done | bytes 1048592 | tf_op jit(solution)/shard_map/all_gather | solution.py:54
  1145.7 2.0 fusion.37
  1147.7 2.0 convolution_add_fusion.8
  1149.7 2.7 convolution_add_fusion.7
  1152.5 30.9 %all-reduce.35.cloned.1.call-done = f32[2,64,256]{2,1,0:T(8,128)} async-done(((f32[2,64,256]{2,1,0:T(8,128)}), f32[2,64,256]{2,1,0:T(8,128)}) %all-reduce.35.cloned.1.call-update) | async-done | bytes 131088 | tf_op jit(solution)/shard_map/psum | solution.py:98
  1183.5 41.2 %all-gather.54.cloned.1.call-done = f32[2,64,2048]{2,1,0:T(8,128)} async-done(((f32[2,64,256]{2,1,0:T(8,128)}), f32[2,64,2048]{2,1,0:T(8,128)}) %all-gather.54.cloned.1.call-update) | async-done | bytes 1048592 | tf_op jit(solution)/shard_map/all_gather | solution.py:54
  1224.7 2.8 fusion.44
  1227.5 30.9 %all-reduce.37.cloned.1.call-done = f32[2,64,256]{2,1,0:T(8,128)} async-done(((f32[2,64,256]{2,1,0:T(8,128)}), f32[2,64,256]{2,1,0:T(8,128)}) %all-reduce.37.cloned.1.call-update) | async-done | bytes 131088 | tf_op jit(solution)/shard_map/psum | solution.py:106
  1263.5 37.0 %all-gather.56.cloned.1.call-done = f32[2,64,2048]{2,1,0:T(8,128)} async-done(((f32[2,64,256]{2,1,0:T(8,128)}), f32[2,64,2048]{2,1,0:T(8,128)}) %all-gather.56.cloned.1.call-update) | async-done | bytes 1048592 | tf_op jit(solution)/shard_map/all_gather | solution.py:54
  1304.3 2.0 convolution_add_fusion.6
  1308.3 2.7 convolution_add_fusion.4
  1311.1 30.9 %all-reduce.39.cloned.1.call-done = f32[2,64,256]{2,1,0:T(8,128)} async-done(((f32[2,64,256]{2,1,0:T(8,128)}), f32[2,64,256]{2,1,0:T(8,128)}) %all-reduce.39.cloned.1.call-update) | async-done | bytes 131088 | tf_op jit(solution)/shard_map/psum | solution.py:98
  1342.0 41.4 %all-gather.58.cloned.1.call-done = f32[2,64,2048]{2,1,0:T(8,128)} async-done(((f32[2,64,256]{2,1,0:T(8,128)}), f32[2,64,2048]{2,1,0:T(8,128)}) %all-gather.58.cloned.1.call-update) | async-done | bytes 1048592 | tf_op jit(solution)/shard_map/all_gather | solution.py:54
  1383.4 2.8 fusion.52
  1386.3 30.9 %all-reduce.41.cloned.1.call-done = f32[2,64,256]{2,1,0:T(8,128)} async-done(((f32[2,64,256]{2,1,0:T(8,128)}), f32[2,64,256]{2,1,0:T(8,128)}) %all-reduce.41.cloned.1.call-update) | async-done | bytes 131088 | tf_op jit(solution)/shard_map/psum | solution.py:106
  1418.8 40.2 %all-gather.60.cloned.1.call-done = f32[2,64,2048]{2,1,0:T(8,128)} async-done(((f32[2,64,256]{2,1,0:T(8,128)}), f32[2,64,2048]{2,1,0:T(8,128)}) %all-gather.60.cloned.1.call-update) | async-done | bytes 1048592 | tf_op jit(solution)/shard_map/all_gather | solution.py:54
  (176 shorter events, 71.6 us)
Async XLA Ops:
  7.2 170.5 %copy-start.4 = (f32[5,2,64,512]{3,2,1,0:T(8,128)S(1)}, f32[5,2,64,512]{3,2,1,0:T(8,128)}, u32[]{:S(2)}) copy-start(f32[5,2,64,512]{3,2,1,0:T(8,128)} %param.6) | copy-start | bytes 3932164
  7.2 22.4 %all-gather.62.cloned.1.call-start = ((), (), s32[]{:S(2)}) async-start(), calls=%async_computation.31 | async-start | bytes 1310720 | tf_op jit(solution)/shard_map/all_gather | solution.py:50
  9.0 95.6 %all-reduce.15.cloned.1.call-start = ((), (), s32[]{:S(2)}) async-start(), calls=%async_computation | async-start | bytes 524288 | tf_op jit(solution)/shard_map/psum | solution.py:69
  32.7 89.9 %all-gather.28.cloned.1.call-start = ((), (), s32[]{:S(2)}) async-start(), calls=%async_computation.1 | async-start | bytes 1310720 | tf_op jit(solution)/shard_map/all_gather | solution.py:50
  106.3 69.5 %all-gather.64.cloned.1.call-start = ((), (), s32[]{:S(2)}) async-start(), calls=%async_computation.32 | async-start | bytes 2359296 | tf_op jit(solution)/shard_map/all_gather | solution.py:61
  126.6 67.2 %all-gather.30.cloned.1.call-start = ((), (), s32[]{:S(2)}) async-start(), calls=%async_computation.2 | async-start | bytes 1310720 | tf_op jit(solution)/shard_map/all_gather | solution.py:50
  178.4 90.2 %all-reduce.17.cloned.1.call-start = ((), (), s32[]{:S(2)}) async-start(), calls=%async_computation.3 | async-start | bytes 524288 | tf_op jit(solution)/shard_map/psum | solution.py:69
  196.9 89.8 %all-gather.32.cloned.1.call-start = ((), (), s32[]{:S(2)}) async-start(), calls=%async_computation.4 | async-start | bytes 1310720 | tf_op jit(solution)/shard_map/all_gather | solution.py:50
  270.4 70.8 %all-gather.66.cloned.1.call-start = ((), (), s32[]{:S(2)}) async-start(), calls=%async_computation.33 | async-start | bytes 2359296 | tf_op jit(solution)/shard_map/all_gather | solution.py:61
  292.0 67.2 %all-gather.34.cloned.1.call-start = ((), (), s32[]{:S(2)}) async-start(), calls=%async_computation.5 | async-start | bytes 1310720 | tf_op jit(solution)/shard_map/all_gather | solution.py:50
  343.8 89.7 %all-reduce.19.cloned.1.call-start = ((), (), s32[]{:S(2)}) async-start(), calls=%async_computation.6 | async-start | bytes 524288 | tf_op jit(solution)/shard_map/psum | solution.py:69
  362.3 89.0 %all-gather.36.cloned.1.call-start = ((), (), s32[]{:S(2)}) async-start(), calls=%async_computation.7 | async-start | bytes 1310720 | tf_op jit(solution)/shard_map/all_gather | solution.py:50
  435.2 70.6 %all-gather.68.cloned.1.call-start = ((), (), s32[]{:S(2)}) async-start(), calls=%async_computation.34 | async-start | bytes 2359296 | tf_op jit(solution)/shard_map/all_gather | solution.py:61
  456.6 67.2 %all-gather.38.cloned.1.call-start = ((), (), s32[]{:S(2)}) async-start(), calls=%async_computation.8 | async-start | bytes 1310720 | tf_op jit(solution)/shard_map/all_gather | solution.py:50
  508.4 89.7 %all-reduce.21.cloned.1.call-start = ((), (), s32[]{:S(2)}) async-start(), calls=%async_computation.9 | async-start | bytes 524288 | tf_op jit(solution)/shard_map/psum | solution.py:69
  527.0 88.9 %all-gather.40.cloned.1.call-start = ((), (), s32[]{:S(2)}) async-start(), calls=%async_computation.10 | async-start | bytes 1310720 | tf_op jit(solution)/shard_map/all_gather | solution.py:50
  599.8 70.6 %all-gather.70.cloned.1.call-start = ((), (), s32[]{:S(2)}) async-start(), calls=%async_computation.35 | async-start | bytes 2359296 | tf_op jit(solution)/shard_map/all_gather | solution.py:61
  620.4 294.4 %copy-start.3 = (f32[2,64,512]{2,1,0:T(8,128)S(1)}, f32[2,64,512]{2,1,0:T(8,128)}, u32[]{:S(2)}) copy-start(f32[2,64,512]{2,1,0:T(8,128)} %get-tuple-element.7) | copy-start | bytes 786436
  621.2 67.2 %all-gather.42.cloned.1.call-start = ((), (), s32[]{:S(2)}) async-start(), calls=%async_computation.11 | async-start | bytes 1310720 | tf_op jit(solution)/shard_map/all_gather | solution.py:50
  673.0 89.7 %all-reduce.23.cloned.1.call-start = ((), (), s32[]{:S(2)}) async-start(), calls=%async_computation.12 | async-start | bytes 524288 | tf_op jit(solution)/shard_map/psum | solution.py:69
  691.5 105.1 %all-reduce.25.cloned.1.call-start = ((), (), s32[]{:S(2)}) async-start(), calls=%async_computation.13 | async-start | bytes 262144 | tf_op jit(solution)/shard_map/psum | solution.py:106
  765.4 303.3 %copy-start.2 = (f32[2,64,512]{2,1,0:T(8,128)S(1)}, f32[2,64,512]{2,1,0:T(8,128)}, u32[]{:S(2)}) copy-start(f32[2,64,512]{2,1,0:T(8,128)} %get-tuple-element.9) | copy-start | bytes 786436
  765.5 72.4 %all-gather.44.cloned.1.call-start = ((), (), s32[]{:S(2)}) async-start(), calls=%async_computation.14 | async-start | bytes 1179648 | tf_op jit(solution)/shard_map/all_gather | solution.py:54
  798.2 75.2 %all-reduce.27.cloned.1.call-start = ((), (), s32[]{:S(2)}) async-start(), calls=%async_computation.15 | async-start | bytes 262144 | tf_op jit(solution)/shard_map/psum | solution.py:98
  842.4 72.4 %all-gather.46.cloned.1.call-start = ((), (), s32[]{:S(2)}) async-start(), calls=%async_computation.16 | async-start | bytes 1179648 | tf_op jit(solution)/shard_map/all_gather | solution.py:54
  873.4 75.2 %all-reduce.29.cloned.1.call-start = ((), (), s32[]{:S(2)}) async-start(), calls=%async_computation.17 | async-start | bytes 262144 | tf_op jit(solution)/shard_map/psum | solution.py:106
  917.6 72.3 %all-gather.48.cloned.1.call-start = ((), (), s32[]{:S(2)}) async-start(), calls=%async_computation.18 | async-start | bytes 1179648 | tf_op jit(solution)/shard_map/all_gather | solution.py:54
  950.1 77.2 %all-reduce.31.cloned.1.call-start = ((), (), s32[]{:S(2)}) async-start(), calls=%async_computation.19 | async-start | bytes 262144 | tf_op jit(solution)/shard_map/psum | solution.py:98
  993.7 231.0 %copy-start.1 = (f32[2,64,512]{2,1,0:T(8,128)S(1)}, f32[2,64,512]{2,1,0:T(8,128)}, u32[]{:S(2)}) copy-start(f32[2,64,512]{2,1,0:T(8,128)} %get-tuple-element.11) | copy-start | bytes 786436
  996.4 72.3 %all-gather.50.cloned.1.call-start = ((), (), s32[]{:S(2)}) async-start(), calls=%async_computation.20 | async-start | bytes 1179648 | tf_op jit(solution)/shard_map/all_gather | solution.py:54
  1027.4 75.0 %all-reduce.33.cloned.1.call-start = ((), (), s32[]{:S(2)}) async-start(), calls=%async_computation.21 | async-start | bytes 262144 | tf_op jit(solution)/shard_map/psum | solution.py:106
  1071.5 72.4 %all-gather.52.cloned.1.call-start = ((), (), s32[]{:S(2)}) async-start(), calls=%async_computation.22 | async-start | bytes 1179648 | tf_op jit(solution)/shard_map/all_gather | solution.py:54
  1104.0 79.3 %all-reduce.35.cloned.1.call-start = ((), (), s32[]{:S(2)}) async-start(), calls=%async_computation.23 | async-start | bytes 262144 | tf_op jit(solution)/shard_map/psum | solution.py:98
  1152.4 72.3 %all-gather.54.cloned.1.call-start = ((), (), s32[]{:S(2)}) async-start(), calls=%async_computation.24 | async-start | bytes 1179648 | tf_op jit(solution)/shard_map/all_gather | solution.py:54
  1183.4 200.0 %copy-start = (f32[2,64,512]{2,1,0:T(8,128)S(1)}, f32[2,64,512]{2,1,0:T(8,128)}, u32[]{:S(2)}) copy-start(f32[2,64,512]{2,1,0:T(8,128)} %get-tuple-element.13) | copy-start | bytes 786436
  1183.4 75.0 %all-reduce.37.cloned.1.call-start = ((), (), s32[]{:S(2)}) async-start(), calls=%async_computation.25 | async-start | bytes 262144 | tf_op jit(solution)/shard_map/psum | solution.py:106
  1227.5 73.0 %all-gather.56.cloned.1.call-start = ((), (), s32[]{:S(2)}) async-start(), calls=%async_computation.26 | async-start | bytes 1179648 | tf_op jit(solution)/shard_map/all_gather | solution.py:54
  1260.0 81.9 %all-reduce.39.cloned.1.call-start = ((), (), s32[]{:S(2)}) async-start(), calls=%async_computation.27 | async-start | bytes 262144 | tf_op jit(solution)/shard_map/psum | solution.py:98
  1262.4 156.4 %copy-start.5 = (f32[2,64,512]{2,1,0:T(8,128)S(1)}, f32[2,64,512]{2,1,0:T(8,128)}, u32[]{:S(2)}) copy-start(f32[2,64,512]{2,1,0:T(8,128)} %all-reduce.23.cloned.1.call-done) | copy-start | bytes 786436
  1311.0 72.4 %all-gather.58.cloned.1.call-start = ((), (), s32[]{:S(2)}) async-start(), calls=%async_computation.28 | async-start | bytes 1179648 | tf_op jit(solution)/shard_map/all_gather | solution.py:54
  1342.0 75.2 %all-reduce.41.cloned.1.call-start = ((), (), s32[]{:S(2)}) async-start(), calls=%async_computation.29 | async-start | bytes 262144 | tf_op jit(solution)/shard_map/psum | solution.py:106
  1386.2 72.9 %all-gather.60.cloned.1.call-start = ((), (), s32[]{:S(2)}) async-start(), calls=%async_computation.30 | async-start | bytes 1179648 | tf_op jit(solution)/shard_map/all_gather | solution.py:54
  1418.8 45.1 %copy-start.6 = (f32[5,2,64,512]{3,2,1,0:T(8,128)}, f32[5,2,64,512]{3,2,1,0:T(8,128)S(1)}, u32[]{:S(2)}) copy-start(f32[5,2,64,512]{3,2,1,0:T(8,128)S(1)} %bitcast_dynamic-update-slice_fusion.5) | copy-start | bytes 3932164
  1464.0 1.1 copy-start.7
Sparse Core Ops, SparseCore 0:
  10.1 19.4 all-gather.61
  33.5 71.0 all-reduce.14
  106.7 15.8 all-gather.27
  126.7 49.0 all-gather.63
  178.5 15.2 all-gather.29
  197.6 70.9 all-reduce.16
  270.7 15.8 all-gather.31
  292.1 49.0 all-gather.65
  343.9 15.2 all-gather.33
  362.4 70.9 all-reduce.18
  435.4 15.8 all-gather.35
  456.7 49.0 all-gather.67
  508.5 15.2 all-gather.37
  527.1 70.9 all-reduce.20
  600.0 15.8 all-gather.39
  621.3 49.0 all-gather.69
  673.1 15.2 all-gather.41
  691.6 70.9 all-reduce.22
  765.6 30.9 all-reduce.24
  798.5 39.3 all-gather.43
  842.5 30.7 all-reduce.26
  875.4 39.3 all-gather.45
  917.7 30.7 all-reduce.28
  950.5 39.3 all-gather.47
  996.5 30.7 all-reduce.30
  1029.3 39.3 all-gather.49
  1071.6 30.7 all-reduce.32
  1104.5 39.3 all-gather.51
  1152.5 30.7 all-reduce.34
  1185.3 39.3 all-gather.53
  1227.6 30.7 all-reduce.36
  1261.1 39.3 all-gather.55
  1311.1 30.7 all-reduce.38
  1344.0 39.3 all-gather.57
  1386.4 30.7 all-reduce.40
  1419.7 39.3 all-gather.59
